TPU v7x, 32 devices: a whole 2x2x4 slice. The times are simulated.
32 devices in a mesh: scen: 8 (over y, x, core), own: 4 (over z).
Axes of the slice: x: 2, y: 2, z: 4, core: 2. Of those that a mesh axis runs over, the one named last changes fastest.
Arguments:
- returns: float32 [8192, 4096], P('scen', 'own'), may hold values from -50 to 50, as said below
Outputs:
- shrunk_cov: float32 [4096, 4096], P('scen', 'own')
Inputs may be any that keep to these rules, and one draw needn't show every extreme that they name: Finite real returns.
All inputs are finite; a program needn't handle non-finite values.
Results may differ from a plain program's by a relative error of at most 0.00014.
Values sent between devices are 32-bit elements; how exact they have to be, the bound alone decides.
A program may use at most 128 MiB of HBM per device.

v0:
```python
import jax
import jax.numpy as jnp
from jax import lax
from jax.sharding import PartitionSpec as P

epsilon = 1e-06


def product_over_scenarios(left_part, right_part):
    return lax.dot_general(
        left_part,
        right_part,
        (((0,), (0,)), ((), ())),
        precision=lax.Precision.HIGHEST,
        preferred_element_type=jnp.float32,
    )


def on_device(returns):
    scen_devices = lax.axis_size("scen")
    own_devices = lax.axis_size("own")
    local_rows = returns.shape[0]
    own_cols = returns.shape[1]
    scenarios = local_rows * scen_devices
    order = own_cols * own_devices
    col_total = lax.psum(jnp.sum(returns, axis=0), "scen")
    centered = returns - col_total / scenarios
    wide_rows = lax.all_gather(centered, "own", axis=1, tiled=True)
    squares = wide_rows * wide_rows
    row_norm = jnp.sum(squares, axis=1)
    beta_local = jnp.sum(row_norm * row_norm)
    trace_sum, beta_raw = lax.psum((jnp.sum(squares), beta_local), "scen")
    gram_tile = lax.psum_scatter(
        product_over_scenarios(wide_rows, centered), "scen", scatter_dimension=0, tiled=True
    )
    covariance = gram_tile / scenarios
    frob_local = jnp.sum(covariance * covariance)
    frob_sum = lax.psum(frob_local, ("scen", "own"))
    target = trace_sum / (scenarios * order)
    beta_term = (beta_raw / scenarios - frob_sum) / (order * scenarios)
    delta_term = (frob_sum - order * target * target) / order
    shrinkage = beta_term / (delta_term + epsilon)
    tile_height = covariance.shape[0]
    row_ids = lax.axis_index("scen") * tile_height + lax.broadcasted_iota(
        jnp.int32, covariance.shape, 0
    )
    col_ids = lax.axis_index("own") * own_cols + lax.broadcasted_iota(
        jnp.int32, covariance.shape, 1
    )
    diag_mask = (row_ids == col_ids).astype(jnp.float32)
    return (1.0 - shrinkage) * covariance + shrinkage * target * diag_mask


def solution(mesh):
    placed = (P("scen", "own"),)
    return jax.shard_map(
        on_device, mesh=mesh, in_specs=placed, out_specs=P("scen", "own"), check_vma=False
    )
```

profile of v0, /device:TPU:0, one launch (start us, length us, event | category | flops | bytes accessed | tf_op | source)
XLA Modules:
  0.0 543.0 jit_solution(2770630650774440942)
XLA Ops:
  6.5 0.0 all-gather.2.cloned.1.call-start
  6.5 2.5 reduce_sum.45
  9.0 15.2 %psum.28 = f32[1024]{0:T(1024)S(1)} all-reduce(f32[1024]{0:T(1024)S(1)} %reduce_sum.45), channel_id=1, replica_groups=mesh['scen'=8,'own'=4] {'scen'}, use_global_device_ids=true, to_apply=%region_1.0 | all-reduce | flops 1024 | bytes 8192 | tf_op jit(solution)/shard_map/psum | solution.py:26
  24.2 5.1 broadcast_subtract_fusion
  29.3 0.0 all-gather.2.cloned.1.call-update
  29.3 0.0 reduce-scatter.2.cloned.1.call-start
  29.3 286.2 %all-gather.2.cloned.1.call-done = f32[1024,4096]{1,0:T(8,128)} async-done(((f32[1024,1024]{1,0:T(8,128)}), f32[1024,4096]{1,0:T(8,128)}) %all-gather.2.cloned.1.call-update) | async-done | bytes 16777232 | tf_op jit(solution)/shard_map/all_gather | solution.py:28
  315.6 59.2 %fusion = f32[4096,1024]{1,0:T(8,128)} fusion(f32[1024,4096]{1,0:T(8,128)} %all-gather.2.cloned.1.call-done, f32[1024,1024]{1,0:T(8,128)} %broadcast_subtract_fusion), kind=kOutput, calls=%fused_computation.9 | convolution fusion | flops 51539607552 | bytes 37748736 | tf_op jit(solution)/shard_map/dot_general | solution.py:10
  374.8 0.0 reduce-scatter.2.cloned.1.call-update
  374.8 12.8 %multiply_reduce_fusion = (f32[]{:T(128)}, f32[1024]{0:T(1024)S(1)}) fusion(f32[1024,4096]{1,0:T(8,128)} %all-gather.2.cloned.1.call-done), kind=kLoop, calls=%fused_computation | loop fusion | flops 12581887 | bytes 16781316 | tf_op jit(solution)/shard_map/reduce_sum | solution.py:32
  387.6 0.6 multiply_reduce_fusion.3
  388.2 14.2 %all-reduce = (f32[]{:T(128)}, f32[]{:T(128)}) all-reduce(f32[]{:T(128)} %multiply_reduce_fusion.3, f32[]{:T(128)} %get-tuple-element.5), channel_id=1, replica_groups=mesh['scen'=8,'own'=4] {'scen'}, use_global_device_ids=true, to_apply=%region_5.0 | all-reduce | flops 2 | bytes 16 | tf_op jit(solution)/shard_map/psum | solution.py:32
  405.0 84.4 %reduce-scatter.2.cloned.1.call-done = f32[512,1024]{1,0:T(8,128)} async-done(((f32[4096,1024]{1,0:T(8,128)}), f32[512,1024]{1,0:T(8,128)}) %reduce-scatter.2.cloned.1.call-update) | async-done | bytes 2097168 | tf_op jit(solution)/shard_map/reduce_scatter | solution.py:33
  489.3 2.7 multiply_reduce_fusion.2
  492.1 39.5 %psum.30 = f32[]{:T(128)} all-reduce(f32[]{:T(128)} %multiply_reduce_fusion.2), channel_id=1, replica_groups=mesh['scen'=8,'own'=4] {'scen','own'}, use_global_device_ids=true, to_apply=%region_7.0 | all-reduce | flops 1 | bytes 8 | tf_op jit(solution)/shard_map/psum | solution.py:38
  532.9 3.2 select_add_fusion
  (3 shorter events, 0.0 us)
Async XLA Ops:
  6.5 309.0 %all-gather.2.cloned.1.call-start = ((), (), s32[]{:S(2)}) async-start(), calls=%async_computation.1 | async-start | bytes 20971520 | tf_op jit(solution)/shard_map/all_gather | solution.py:28
  29.3 460.0 %reduce-scatter.2.cloned.1.call-start = ((), (), s32[]{:S(2)}) async-start(), calls=%async_computation.2 | async-start | bytes 18874368 | tf_op jit(solution)/shard_map/reduce_scatter | solution.py:33
Sparse Core Ops, SparseCore 0:
  29.4 286.1 all-gather.1
  374.9 114.3 reduce-scatter.1
where the time goes:
time: 543 us
  waiting for transfers between devices  371 us (68%)
  blocking collectives  68.9 us (13%)
  matrix products  59.2 us (11%)
  other arithmetic  27 us (5%)
  between operations  17.3 us (3%)
    all_gather x1, waiting for transfers between devices, on_device(): wide_rows = lax.all_gather(centered, 'own', axis=1, tiled=True)  286 us
    reduce_scatter x1, waiting for transfers between devices, on_device(): lax.psum_scatter(product_over_scenarios(wide_rows, centered), 'scen', sca...  84.4 us
    dot_general x1, matrix products, product_over_scenarios(): lax.dot_general(left_part, right_part, (((0,), (0,)), ((), ())), precisio...  59.2 us
    psum x1, blocking collectives, on_device(): frob_sum = lax.psum(frob_local, ('scen', 'own'))  39.5 us
    psum x1, blocking collectives, on_device(): col_total = lax.psum(jnp.sum(returns, axis=0), 'scen')  15.2 us
    psum x1, blocking collectives, on_device(): trace_sum, beta_raw = lax.psum((jnp.sum(squares), beta_local), 'scen')  14.2 us
    reduce_sum x1, other arithmetic, on_device(): trace_sum, beta_raw = lax.psum((jnp.sum(squares), beta_local), 'scen')  12.8 us
  transfers between devices with their start and end apart: 2, of which 2 were waited for; matrix products, arithmetic and copies ran while one was open for 2% of the time, Pallas kernels for 0%

commit v1 on v0

--- a/solution.py
+++ b/solution.py
@@ -25,7 +25,7 @@
     order = own_cols * own_devices
     col_total = lax.psum(jnp.sum(returns, axis=0), "scen")
     centered = returns - col_total / scenarios
-    wide_rows = lax.all_gather(centered, "own", axis=1, tiled=True)
+    wide_rows = jnp.concatenate(lax.all_gather(centered, "own"), axis=1)
     squares = wide_rows * wide_rows
     row_norm = jnp.sum(squares, axis=1)
     beta_local = jnp.sum(row_norm * row_norm)

time: 543 us -> 561 us (1.033)
  local copies, waits for them, and re-layouts: 0 us -> 16.4 us
    reshape x0 -> x1, local copies, waits for them, and re-layouts: none -> 16.4 us  [on_device(): wide_rows = jnp.concatenate(lax.all_gather(centered, 'own'), axis=1)]
where the time goes in v1:
time: 561 us
  waiting for transfers between devices  371 us (66%)
  blocking collectives  68.9 us (12%)
  matrix products  59.9 us (11%)
  other arithmetic  26.9 us (5%)
  between operations  17.3 us (3%)
  local copies, waits for them, and re-layouts  16.4 us (3%)
    all_gather x1, waiting for transfers between devices, on_device(): wide_rows = jnp.concatenate(lax.all_gather(centered, 'own'), axis=1)  286 us
    reduce_scatter x1, waiting for transfers between devices, on_device(): lax.psum_scatter(product_over_scenarios(wide_rows, centered), 'scen', sca...  84.9 us
    dot_general x1, matrix products, product_over_scenarios(): lax.dot_general(left_part, right_part, (((0,), (0,)), ((), ())), precisio...  59.9 us
    psum x1, blocking collectives, on_device(): frob_sum = lax.psum(frob_local, ('scen', 'own'))  39.5 us
    reshape x1, local copies, waits for them, and re-layouts, on_device(): wide_rows = jnp.concatenate(lax.all_gather(centered, 'own'), axis=1)  16.4 us
    psum x1, blocking collectives, on_device(): col_total = lax.psum(jnp.sum(returns, axis=0), 'scen')  15.2 us
    psum x1, blocking collectives, on_device(): trace_sum, beta_raw = lax.psum((jnp.sum(squares), beta_local), 'scen')  14.2 us
    reduce_sum x1, other arithmetic, on_device(): trace_sum, beta_raw = lax.psum((jnp.sum(squares), beta_local), 'scen')  12.8 us
  transfers between devices with their start and end apart: 2, of which 2 were waited for; matrix products, arithmetic and copies ran while one was open for 2% of the time, Pallas kernels for 0%

profile of v1, /device:TPU:0, one launch (start us, length us, event | category | flops | bytes accessed | tf_op | source)
XLA Modules:
  0.0 560.6 jit_solution(3455217905758647225)
XLA Ops:
  6.5 0.0 all-gather.3.cloned.1.call-start
  6.5 2.5 reduce_sum.45
  9.0 15.2 %psum.28 = f32[1024]{0:T(1024)S(1)} all-reduce(f32[1024]{0:T(1024)S(1)} %reduce_sum.45), channel_id=1, replica_groups=mesh['scen'=8,'own'=4] {'scen'}, use_global_device_ids=true, to_apply=%region_1.0 | all-reduce | flops 1024 | bytes 8192 | tf_op jit(solution)/shard_map/psum | solution.py:26
  24.2 5.1 broadcast_subtract_fusion
  29.2 0.0 all-gather.3.cloned.1.call-update
  29.3 0.0 reduce-scatter.2.cloned.1.call-start
  29.3 286.2 %all-gather.3.cloned.1.call-done = f32[4096,1024]{1,0:T(8,128)} async-done(((f32[1024,1024]{1,0:T(8,128)}), f32[4096,1024]{1,0:T(8,128)}) %all-gather.3.cloned.1.call-update) | async-done | bytes 16777232 | tf_op jit(solution)/shard_map/all_gather | solution.py:28
  315.5 16.4 %copy.2 = f32[1024,4,1024]{0,2,1:T(8,128)} copy(f32[1024,4,1024]{2,0,1:T(8,128)} %bitcast.6) | data formatting | bytes 33554432 | tf_op jit(solution)/shard_map/reshape | solution.py:28
  331.9 59.9 %fusion = f32[4096,1024]{1,0:T(8,128)} fusion(f32[1024,4096]{0,1:T(8,128)} %bitcast.8, f32[1024,1024]{1,0:T(8,128)} %broadcast_subtract_fusion), kind=kOutput, calls=%fused_computation.9 | convolution fusion | flops 51539607552 | bytes 37748736 | tf_op jit(solution)/shard_map/dot_general | solution.py:10
  391.8 0.0 reduce-scatter.2.cloned.1.call-update
  391.9 12.8 %multiply_reduce_fusion = (f32[]{:T(128)}, f32[1024]{0:T(1024)S(1)}) fusion(f32[1024,4,1024]{2,0,1:T(8,128)} %bitcast.7), kind=kLoop, calls=%fused_computation | loop fusion | flops 12581887 | bytes 16781316 | tf_op jit(solution)/shard_map/reduce_sum | solution.py:32
  404.7 0.6 multiply_reduce_fusion.3
  405.3 14.2 %all-reduce = (f32[]{:T(128)}, f32[]{:T(128)}) all-reduce(f32[]{:T(128)} %multiply_reduce_fusion.3, f32[]{:T(128)} %get-tuple-element.5), channel_id=1, replica_groups=mesh['scen'=8,'own'=4] {'scen'}, use_global_device_ids=true, to_apply=%region_5.0 | all-reduce | flops 2 | bytes 16 | tf_op jit(solution)/shard_map/psum | solution.py:32
  421.5 84.9 %reduce-scatter.2.cloned.1.call-done = f32[512,1024]{1,0:T(8,128)} async-done(((f32[4096,1024]{1,0:T(8,128)}), f32[512,1024]{1,0:T(8,128)}) %reduce-scatter.2.cloned.1.call-update) | async-done | bytes 2097168 | tf_op jit(solution)/shard_map/reduce_scatter | solution.py:33
  506.4 2.7 multiply_reduce_fusion.2
  509.7 39.5 %psum.30 = f32[]{:T(128)} all-reduce(f32[]{:T(128)} %multiply_reduce_fusion.2), channel_id=1, replica_groups=mesh['scen'=8,'own'=4] {'scen','own'}, use_global_device_ids=true, to_apply=%region_7.0 | all-reduce | flops 1 | bytes 8 | tf_op jit(solution)/shard_map/psum | solution.py:38
  550.6 3.2 select_add_fusion
  (3 shorter events, 0.0 us)
Async XLA Ops:
  6.5 309.0 %all-gather.3.cloned.1.call-start = ((), (), s32[]{:S(2)}) async-start(), calls=%async_computation.2 | async-start | bytes 20971520 | tf_op jit(solution)/shard_map/all_gather | solution.py:28
  29.3 477.1 %reduce-scatter.2.cloned.1.call-start = ((), (), s32[]{:S(2)}) async-start(), calls=%async_computation.1 | async-start | bytes 18874368 | tf_op jit(solution)/shard_map/reduce_scatter | solution.py:33
Sparse Core Ops, SparseCore 0:
  29.4 286.1 all-gather.2
  391.9 114.3 reduce-scatter.1
